TPU v7x, 32 devices: a whole 2x2x4 slice. The times are simulated.
32 devices in a mesh: grp: 2 (over y), kvp: 4 (over x, core), tp: 4 (over z).
Axes of the slice: x: 2, y: 2, z: 4, core: 2. Of those that a mesh axis runs over, the one named last changes fastest.
Arguments:
- normed: bfloat16 [512, 6144], P('grp', 'kvp'), parts along dimension 0, may hold values from -6 to 6
- w_query: bfloat16 [6144, 6144], P('kvp', 'tp'), may hold values from -0.078125 to 0.078125
- w_key: bfloat16 [6144, 1024], P('kvp', 'tp'), may hold values from -0.078125 to 0.078125
- w_value: bfloat16 [6144, 1024], P('kvp', 'tp'), may hold values from -0.078125 to 0.078125
- w_out: bfloat16 [6144, 6144], P('tp', 'kvp'), may hold values from -0.078125 to 0.078125
- key_cache: bfloat16 [8, 1024, 128, 128], P('tp', ('grp', 'kvp')), parts along dimension 1, may hold values from -128 to 128
- value_cache: bfloat16 [8, 1024, 128, 128], P('tp', ('grp', 'kvp')), parts along dimension 1, may hold values from -6 to 6
- lengths: int32 [512], P('grp'), parts along dimension 0, may hold values from 1 to 12288, as said below
- page_table: int32 [512, 96], P('grp'), parts along dimension 0, may hold values from -1 to 511, as said below
Outputs:
- attended: bfloat16 [512, 6144], P(('grp', 'tp'), 'kvp'), parts along dimension 0
There are 2 independent parts, one for each index of `grp`. A program takes and returns all parts, laid end to end along the dimension named above; an argument that names none is the same for every part. Nothing has to cross between parts.
Inputs may be any that keep to these rules, and one draw needn't show every extreme that they name: `lengths`: every request has at least one cached token; the longest request fills all 96 entries of its page table. `page_table`: entry [b, j] is a page index exactly when j < ceil(lengths[b] / 128), else -1; no page is named twice. Index kvp = i holds pages i * 128 to (i + 1) * 128 - 1; the pages in use are spread unevenly over kvp.
All inputs are finite; a program needn't handle non-finite values.
Results may differ from a plain program's by a relative error of at most 0.012.
Values may be sent and summed in bfloat16 or wider, within the bound.
A program may use at most 64 MiB of HBM per device.

v0:
```python
import jax
import jax.numpy as jnp
from jax import lax
from jax.sharding import PartitionSpec as P

ROPE_BASE = 1000000.0
NEG = -1e30
TWO_PI_HIGH = 6.28125
TWO_PI_LOW = 0.0019353071795864768


def rotate(x, pos):
    width = x.shape[-1]
    half = width // 2
    freq = ROPE_BASE ** (-(2.0 * jnp.arange(half, dtype=jnp.float32)) / width)
    coarse = lax.optimization_barrier(freq.astype(jnp.bfloat16)).astype(jnp.float32)
    fine = freq - coarse
    pos_e = pos[..., None]
    exact = pos_e * coarse
    turns = jnp.floor(exact / TWO_PI_HIGH)
    angle = exact - turns * TWO_PI_HIGH - turns * TWO_PI_LOW + pos_e * fine
    cosine = jnp.cos(angle)
    sine = jnp.sin(angle)
    first = x[..., :half]
    second = x[..., half:]
    return jnp.concatenate(
        [first * cosine - second * sine, second * cosine + first * sine], axis=-1
    )


def source_merge(received):
    marks, totals, accs = received
    top = jnp.max(marks, axis=0)
    weight = jnp.exp(marks - top[None])
    return (top, jnp.sum(weight * totals, axis=0), jnp.sum(weight[..., None] * accs, axis=0))


def finish(top, total, acc, q_rows, k_rows, v_rows, scale):
    s_new = jnp.einsum("bhgd,bhd->bhg", q_rows, k_rows, preferred_element_type=jnp.float32) * scale
    peak = jnp.maximum(top, s_new)
    w_old = jnp.exp(top - peak)
    w_new = jnp.exp(s_new - peak)
    total = w_old * total + w_new
    acc = w_old[..., None] * acc + w_new[..., None] * v_rows.astype(jnp.float32)[:, :, None, :]
    out = (acc / total[..., None]).astype(jnp.bfloat16)
    return out.reshape(out.shape[0], -1)


def body(normed, w_query, w_key, w_value, w_out, key_cache, value_cache, lengths, page_table):
    batch = normed.shape[0]
    kv_local = key_cache.shape[0]
    pages = key_cache.shape[1]
    page = key_cache.shape[2]
    head_dim = key_cache.shape[3]
    group = w_query.shape[1] // (kv_local * head_dim)
    blocks_max = page_table.shape[1]
    scale = head_dim ** (-0.5)
    rank = lax.axis_index("kvp")
    spread = lax.axis_size("kvp")
    rows = batch // spread
    start = rank * rows
    part_q = jnp.dot(normed, w_query, preferred_element_type=jnp.float32)
    part_k = jnp.dot(normed, w_key, preferred_element_type=jnp.float32)
    part_v = jnp.dot(normed, w_value, preferred_element_type=jnp.float32)
    position = lengths.astype(jnp.float32)
    q_share, k_share, v_share = (
        lax.psum_scatter(part_q, "kvp", scatter_dimension=0, tiled=True),
        lax.psum_scatter(part_k, "kvp", scatter_dimension=0, tiled=True),
        lax.psum_scatter(part_v, "kvp", scatter_dimension=0, tiled=True),
    )
    pos_share = lax.dynamic_slice_in_dim(position, start, rows, 0)
    q_part = rotate(
        q_share.reshape(rows, kv_local, group, head_dim), pos_share[:, None, None]
    ).astype(jnp.bfloat16)
    k_rows = rotate(k_share.reshape(rows, kv_local, head_dim), pos_share[:, None]).astype(
        jnp.bfloat16
    )
    v_rows = v_share.reshape(rows, kv_local, head_dim).astype(jnp.bfloat16)
    q_rot = lax.all_gather(q_part, "kvp", axis=0, tiled=True)
    slot_ids = rank * pages + jnp.arange(pages, dtype=jnp.int32)
    hits = page_table[:, :, None] == slot_ids[None, None, :]
    present = jnp.any(hits, axis=(0, 1))
    request_ids = jnp.arange(batch, dtype=jnp.int32)
    owner = jnp.sum(jnp.where(hits, request_ids[:, None, None], 0), axis=(0, 1))
    block = jnp.sum(
        jnp.where(hits, jnp.arange(blocks_max, dtype=jnp.int32)[None, :, None], 0), axis=(0, 1)
    )
    q_owned = q_rot[owner]
    token_pos = block[:, None] * page + jnp.arange(page, dtype=jnp.int32)[None, :]
    valid = present[:, None] & (token_pos < lengths[owner][:, None])
    scores = (
        jnp.einsum("phgd,hptd->phgt", q_owned, key_cache, preferred_element_type=jnp.float32)
        * scale
    )
    scores = jnp.where(valid[:, None, None, :], scores, NEG)
    slot_top = jnp.max(scores, axis=-1)
    weights = jnp.where(valid[:, None, None, :], jnp.exp(scores - slot_top[..., None]), 0.0)
    slot_total = jnp.sum(weights, axis=-1)
    slot_acc = jnp.einsum(
        "phgt,hptd->phgd",
        weights.astype(jnp.bfloat16),
        value_cache,
        preferred_element_type=jnp.float32,
    )
    belongs = (owner[None, :] == request_ids[:, None]) & present[None, :]
    mask = belongs[:, :, None, None]
    top = jnp.max(jnp.where(mask, slot_top[None], NEG), axis=1)
    factor = jnp.where(mask, jnp.exp(slot_top[None] - top[:, None]), 0.0)
    total = jnp.sum(factor * slot_total[None], axis=1)
    acc = jnp.einsum("bphg,phgd->bhgd", factor, slot_acc, precision=lax.Precision.HIGHEST)
    top, total, acc = source_merge(
        (
            lax.all_to_all(top[None], "kvp", split_axis=1, concat_axis=0, tiled=True),
            lax.all_to_all(total[None], "kvp", split_axis=1, concat_axis=0, tiled=True),
            lax.all_to_all(acc[None], "kvp", split_axis=1, concat_axis=0, tiled=True),
        )
    )
    q_rows = lax.dynamic_slice_in_dim(q_rot, start, rows, 0)
    head_out = finish(top, total, acc, q_rows, k_rows, v_rows, scale)
    terms = jnp.dot(
        lax.all_gather(head_out, "kvp", axis=0, tiled=True),
        w_out,
        preferred_element_type=jnp.float32,
    )
    return lax.psum_scatter(terms, "tp", scatter_dimension=0, tiled=True).astype(jnp.bfloat16)


def solution(mesh):
    return jax.shard_map(
        body,
        mesh=mesh,
        in_specs=(
            P("grp", "kvp"),
            P("kvp", "tp"),
            P("kvp", "tp"),
            P("kvp", "tp"),
            P("tp", "kvp"),
            P("tp", ("grp", "kvp"), None, None),
            P("tp", ("grp", "kvp"), None, None),
            P("grp"),
            P("grp", None),
        ),
        out_specs=P(("grp", "tp"), "kvp"),
        check_vma=False,
    )
```

profile of v0, /device:TPU:0, one launch (start us, length us, event | category | flops | bytes accessed | tf_op | source)
XLA Modules:
  0.0 187.5 jit_solution(7497890433573598699)
XLA Ops:
  6.5 1.1 copy-done
  7.7 2.2 %fusion.49 = f32[256,256]{1,0:T(8,128)} fusion(bf16[256,1536]{1,0:T(8,128)(2,1)S(1)} %copy-done, bf16[1536,256]{1,0:T(8,128)(2,1)} %param.11), kind=kOutput, calls=%fused_computation.77 | convolution fusion | flops 201326592 | bytes 1835008 | tf_op jit(solution)/shard_map/dot_general | solution.py:63
  9.9 0.0 reduce-scatter.5.cloned.1.call-start
  9.9 4.9 %fusion.48 = f32[256,1536]{1,0:T(8,128)} fusion(bf16[256,1536]{1,0:T(8,128)(2,1)S(1)} %copy-done, bf16[1536,1536]{1,0:T(8,128)(2,1)} %param.10), kind=kOutput, calls=%fused_computation.76 | convolution fusion | flops 1207959552 | bytes 7077888 | tf_op jit(solution)/shard_map/dot_general | solution.py:62
  14.9 0.0 reduce-scatter.9.cloned.1.call-start
  14.9 1.0 copy-done.2
  15.9 1.1 fusion.50
  17.1 0.1 copy.63
  17.2 4.6 %fusion.1 = (s32[128]{0:T(128)S(1)}, s32[128]{0:T(128)S(1)}) fusion(s32[128]{0:T(128)S(1)} %iota_add_fusion, s32[256,96]{1,0:T(8,128)S(1)} %copy.63), kind=kLoop, calls=%fused_computation.6 | loop fusion | flops 15728384 | bytes 99840 | tf_op jit(solution)/shard_map/reduce_sum | solution.py:85
  21.8 4.5 %compare_reduce_fusion = pred[128]{0:T(512)(128)(4,1)S(1)} fusion(s32[128]{0:T(128)S(1)} %iota_add_fusion, s32[256,96]{1,0:T(8,128)S(1)} %copy.63), kind=kLoop, calls=%fused_computation.3 | loop fusion | flops 6291328 | bytes 98944 | tf_op jit(solution)/shard_map/reduce_or | solution.py:82
  26.3 1.3 gather_fusion
  27.7 0.1 dynamic_slice.6
  27.7 0.1 fusion.30
  27.9 0.2 fusion.37
  28.1 4.7 %reduce-scatter.7.cloned.1.call-done = f32[64,256]{1,0:T(8,128)} async-done(((f32[256,256]{1,0:T(8,128)}), f32[64,256]{1,0:T(8,128)}) %reduce-scatter.7.cloned.1.call-update) | async-done | bytes 65552 | tf_op jit(solution)/shard_map/reduce_scatter | solution.py:68
  32.8 0.9 reshape.362
  33.7 29.7 %reduce-scatter.5.cloned.1.call-done = f32[64,1536]{1,0:T(8,128)} async-done(((f32[256,1536]{1,0:T(8,128)}), f32[64,1536]{1,0:T(8,128)}) %reduce-scatter.5.cloned.1.call-update) | async-done | bytes 393232 | tf_op jit(solution)/shard_map/reduce_scatter | solution.py:67
  63.4 1.1 reshape.361
  64.6 0.2 subtract_convert_fusion
  64.8 0.2 pad_maximum_fusion
  65.0 0.2 copy.64
  65.2 8.0 %all_gather.6 = bf16[256,2,6,128]{3,1,2,0:T(2,128)(2,1)S(1)} all-gather(bf16[64,2,6,128]{3,1,2,0:T(2,128)(2,1)S(1)} %copy.64), channel_id=1, replica_groups=mesh['grp'=2,'kvp'=4,'tp'=4] {'kvp'}, dimensions={0}, use_global_device_ids=true | all-gather | bytes 983040 | tf_op jit(solution)/shard_map/all_gather | solution.py:79
  73.2 1.4 gather_fusion.1
  74.6 7.0 %fusion.47 = (f32[128,2,6]{2,1,0:T(2,128)S(1)}, f32[128,2,6,128]{3,2,1,0:T(8,128)S(1)}) fusion(bf16[2,128,128,128]{3,2,1,0:T(8,128)(2,1)} %param.14, bf16[128,2,6,128]{3,1,2,0:T(2,128)(2,1)S(1)} %gather_fusion.1, pred[128,128]{1,0:T(8,128)(4,1)S(1)} %fusion.30), kind=kOutput, calls=%fused_computation.75 | convolution fusion | flops 50919936 | bytes 9590784 | tf_op jit(solution)/shard_map/phgd,hptd->phgt/dot_general | solution.py:92
  81.6 0.1 copy.67
  81.7 0.8 fusion.14
  82.5 0.1 copy.78
  82.6 0.5 select_reduce_fusion
  83.1 0.9 multiply_reduce_fusion
  84.0 0.2 copy.79
  84.2 1.0 reshape.384
  85.1 3.3 %all-to-all-start.2 = ((f32[4,1,768]{2,1,0:T(1,128)}), f32[4,1,768]{2,1,0:T(1,128)S(1)}, u32[]{:S(2)}, u32[]{:S(2)}) async-start(f32[4,1,768]{2,1,0:T(1,128)} %reshape.384), calls=%async_computation.5 | async-start | bytes 24576 | tf_op jit(solution)/shard_map/all_to_all | solution.py:114
  88.4 6.7 %fusion.2 = f32[128,2,6,128]{3,2,1,0:T(8,128)} fusion(bf16[2,128,128,128]{3,2,1,0:T(8,128)(2,1)} %param.15, f32[128,2,6,128]{3,2,1,0:T(8,128)S(1)} %get-tuple-element.19, f32[128,2,6]{2,1,0:T(2,128)S(1)} %get-tuple-element.18, pred[128,128]{1,0:T(8,128)(4,1)S(1)} %fusion.30), kind=kOutput, calls=%fused_computation.7 | convolution fusion | flops 50921472 | bytes 9984000 | tf_op jit(solution)/shard_map/phgt,hptd->phgd/dot_general | solution.py:99
  95.1 0.2 copy.68
  95.3 1.0 reshape.382
  96.2 3.4 %all-to-all-start = ((f32[4,1,768]{2,1,0:T(1,128)}), f32[4,1,768]{2,1,0:T(1,128)S(1)}, u32[]{:S(2)}, u32[]{:S(2)}) async-start(f32[4,1,768]{2,1,0:T(1,128)} %reshape.382), calls=%async_computation.1 | async-start | bytes 24576 | tf_op jit(solution)/shard_map/all_to_all | solution.py:113
  99.7 3.4 %fusion.7 = f32[1,256,2,6,128]{1,4,3,2,0:T(8,128)S(1)} fusion(f32[128,2,6,128]{3,2,1,0:T(8,128)} %fusion.2, f32[256,2,6]{0,2,1:T(8,128)S(1)} %select_reduce_fusion, f32[128,2,6]{0,2,1:T(8,128)S(1)} %copy.67, pred[256,128]{1,0:T(8,128)(4,1)S(1)} %fusion.28), kind=kOutput, calls=%fused_computation.16 | convolution fusion | flops 604766208 | bytes 2410496 | tf_op jit(solution)/shard_map/bphg,phgd->bhgd/dot_general | solution.py:110
  103.1 2.2 %copy.74 = f32[1,256,2,6,128]{4,2,3,0,1:T(2,128)} copy(f32[1,256,2,6,128]{1,4,3,2,0:T(8,128)S(1)} %fusion.7) | data formatting | bytes 3145728 | tf_op jit(solution)/shard_map/broadcast_in_dim | solution.py:115
  105.2 3.6 %all-to-all-start.1 = ((f32[1,256,2,6,128]{4,2,3,0,1:T(2,128)}), f32[1,256,2,6,128]{4,2,3,0,1:T(2,128)S(1)}, u32[]{:S(2)}, u32[]{:S(2)}) async-start(f32[1,256,2,6,128]{4,2,3,0,1:T(2,128)} %copy.74), calls=%async_computation.3 | async-start | bytes 3145728 | tf_op jit(solution)/shard_map/all_to_all | solution.py:115
  108.9 0.2 subtract_convert_fusion.1
  109.0 0.1 maximum_bitcast_fusion
  109.2 0.8 copy_bitcast_fusion
  110.0 0.1 constant_dynamic-slice_fusion
  110.2 0.3 fusion.26
  110.4 0.1 copy.85
  110.5 0.5 broadcast.314
  111.1 0.7 reduce
  111.7 0.4 reshape.385
  112.2 0.1 copy.87
  112.3 0.7 reduce.1
  113.0 0.4 reshape.383
  113.4 0.1 copy.86
  113.5 0.2 reduce_max.29
  113.7 0.1 copy.88
  113.9 14.9 %all-to-all-done.1 = f32[1,256,2,6,128]{4,2,3,0,1:T(2,128)S(1)} async-done(((f32[1,256,2,6,128]{4,2,3,0,1:T(2,128)}), f32[1,256,2,6,128]{4,2,3,0,1:T(2,128)S(1)}, u32[]{:S(2)}, u32[]{:S(2)}) %all-to-all-start.1) | async-done | bytes 1572896 | tf_op jit(solution)/shard_map/all_to_all | solution.py:115
  128.8 0.1 copy.75
  129.0 0.5 multiply_reduce_fusion.1
  129.4 0.4 divide_convert_fusion
  129.8 0.1 copy.82
  130.0 0.2 convert_element_type.52
  130.2 7.9 %all_gather.7 = bf16[256,1536]{1,0:T(8,128)(2,1)S(1)} all-gather(bf16[64,1536]{1,0:T(8,128)(2,1)S(1)} %convert_element_type.52), channel_id=1, replica_groups=mesh['grp'=2,'kvp'=4,'tp'=4] {'kvp'}, dimensions={0}, use_global_device_ids=true | all-gather | bytes 983040 | tf_op jit(solution)/shard_map/all_gather | solution.py:121
  138.1 4.9 %fusion.51 = f32[256,1536]{1,0:T(8,128)} fusion(bf16[256,1536]{1,0:T(8,128)(2,1)S(1)} %all_gather.7, bf16[1536,1536]{1,0:T(8,128)(2,1)} %param.13), kind=kOutput, calls=%fused_computation.79 | convolution fusion | flops 1207959552 | bytes 7077888 | tf_op jit(solution)/shard_map/dot_general | solution.py:120
  143.0 36.3 %reduce-scatter.11.cloned.1.call-done = f32[64,1536]{1,0:T(8,128)} async-done(((f32[256,1536]{1,0:T(8,128)}), f32[64,1536]{1,0:T(8,128)}) %reduce-scatter.11.cloned.1.call-update) | async-done | bytes 393232 | tf_op jit(solution)/shard_map/reduce_scatter | solution.py:125
  179.3 1.7 convert_element_type.53
  (29 shorter events, 0.3 us)
Async XLA Ops:
  6.5 1.1 copy-start
  6.5 26.3 %reduce-scatter.7.cloned.1.call-start = ((), (), s32[]{:S(2)}) async-start(), calls=%async_computation.8 | async-start | bytes 327680 | tf_op jit(solution)/shard_map/reduce_scatter | solution.py:68
  9.9 53.6 %reduce-scatter.5.cloned.1.call-start = ((), (), s32[]{:S(2)}) async-start(), calls=%async_computation.7 | async-start | bytes 1966080 | tf_op jit(solution)/shard_map/reduce_scatter | solution.py:67
  14.8 1.1 copy-start.2
  14.8 2.3 %copy-start.3 = (s32[256,96]{0,1:T(8,128)S(1)}, s32[256,96]{0,1:T(8,128)}, u32[]{:S(2)}) copy-start(s32[256,96]{0,1:T(8,128)} %param.17) | copy-start | bytes 294916
  14.8 11.5 %copy-start.1 = (s32[256]{0:T(256)S(1)}, s32[256]{0:T(256)}, u32[]{:S(2)}) copy-start(s32[256]{0:T(256)} %param.16) | copy-start | bytes 3076
  14.9 94.3 %reduce-scatter.9.cloned.1.call-start = ((), (), s32[]{:S(2)}) async-start(), calls=%async_computation.9 | async-start | bytes 327680 | tf_op jit(solution)/shard_map/reduce_scatter | solution.py:69
  85.1 11.1 %all-to-all-start.2 = ((f32[4,1,768]{2,1,0:T(1,128)}), f32[4,1,768]{2,1,0:T(1,128)S(1)}, u32[]{:S(2)}, u32[]{:S(2)}) async-start(f32[4,1,768]{2,1,0:T(1,128)} %reshape.384), calls=%async_computation.5 | async-start | bytes 24576 | tf_op jit(solution)/shard_map/all_to_all | solution.py:114
  96.2 9.0 %all-to-all-start = ((f32[4,1,768]{2,1,0:T(1,128)}), f32[4,1,768]{2,1,0:T(1,128)S(1)}, u32[]{:S(2)}, u32[]{:S(2)}) async-start(f32[4,1,768]{2,1,0:T(1,128)} %reshape.382), calls=%async_computation.1 | async-start | bytes 24576 | tf_op jit(solution)/shard_map/all_to_all | solution.py:113
  105.2 23.6 %all-to-all-start.1 = ((f32[1,256,2,6,128]{4,2,3,0,1:T(2,128)}), f32[1,256,2,6,128]{4,2,3,0,1:T(2,128)S(1)}, u32[]{:S(2)}, u32[]{:S(2)}) async-start(f32[1,256,2,6,128]{4,2,3,0,1:T(2,128)} %copy.74), calls=%async_computation.3 | async-start | bytes 3145728 | tf_op jit(solution)/shard_map/all_to_all | solution.py:115
  108.8 70.5 %reduce-scatter.11.cloned.1.call-start = ((), (), s32[]{:S(2)}) async-start(), calls=%async_computation.10 | async-start | bytes 1966080 | tf_op jit(solution)/shard_map/reduce_scatter | solution.py:125
Sparse Core Ops, SparseCore 0:
  10.0 22.7 reduce-scatter.6
  35.4 28.0 reduce-scatter.4
  65.9 20.0 reduce-scatter.8
  143.1 36.0 reduce-scatter.10
where the time goes:
time: 188 us; the launch traced here: 187 us
  waiting for transfers between devices  85.7 us (46%)
  matrix products  30.4 us (16%)
  other arithmetic  17.4 us (9%)
  blocking collectives  15.9 us (8%)
  local copies, waits for them, and re-layouts  14.2 us (8%)
  between operations  13.5 us (7%)
  starting transfers between devices  10.4 us (6%)
    reduce_scatter x1, waiting for transfers between devices, body(): lax.psum_scatter(terms, 'tp', scatter_dimension=0, tiled=True)  36.3 us
    reduce_scatter x1, waiting for transfers between devices, body(): lax.psum_scatter(part_q, 'kvp', scatter_dimension=0, tiled=True)  29.7 us
    all_to_all x1, waiting for transfers between devices, body(): lax.all_to_all(acc[None], 'kvp', split_axis=1, concat_axis=0, tiled=True)  14.9 us
    all_gather x1, blocking collectives, body(): q_rot = lax.all_gather(q_part, 'kvp', axis=0, tiled=True)  8.04 us
    all_gather x1, blocking collectives, body(): lax.all_gather(head_out, 'kvp', axis=0, tiled=True)  7.9 us
    dot_general x1, matrix products, body(): jnp.einsum('phgd,hptd->phgt', q_owned, key_cache, preferred_element_type=...  6.99 us
    dot_general x1, matrix products, body(): jnp.einsum('phgt,hptd->phgd', weights.astype(jnp.bfloat16), value_cache,...  6.71 us
    unnamed x14, local copies, waits for them, and re-layouts  5.09 us
  transfers between devices with their start and end apart: 7, of which 4 were waited for; matrix products, arithmetic and copies ran while one was open for 26% of the time, Pallas kernels for 0%

commit v1 on v0

v1 whole, which is shorter than its diff:
```python
import functools

import jax
import jax.numpy as jnp
from jax import lax
from jax.experimental import pallas as pl
from jax.experimental.pallas import tpu as pltpu
from jax.sharding import PartitionSpec as P

ROPE_BASE = 1000000.0
NEG = -1e30
TWO_PI_HIGH = 6.28125
TWO_PI_LOW = 0.0019353071795864768
MESH = pl.DeviceIdType.MESH
VMEM_LIMIT = 60 * 1024 * 1024


def angles(pos, width):
    half = width // 2
    freq = ROPE_BASE ** (-(2.0 * jnp.arange(half, dtype=jnp.float32)) / width)
    coarse = lax.optimization_barrier(freq.astype(jnp.bfloat16)).astype(jnp.float32)
    fine = freq - coarse
    pos_e = pos[..., None]
    exact = pos_e * coarse
    turns = jnp.floor(exact / TWO_PI_HIGH)
    angle = exact - turns * TWO_PI_HIGH - turns * TWO_PI_LOW + pos_e * fine
    cosine = jnp.cos(angle)
    sine = jnp.sin(angle)
    return (
        jnp.concatenate([cosine, cosine], axis=-1),
        jnp.concatenate([-sine, sine], axis=-1),
    )


def chunks_of(count, most):
    size = most
    while count % size:
        size -= 1
    return [(start, size) for start in range(0, count, size)]


def place(m):
    me = lax.axis_index("kvp")
    core = me % 2
    chip = me // 2
    partner = chip * 2 + (1 - core)
    peers = [((chip + s) % m) * 2 + core for s in range(1, m)]
    return core, partner, peers


def remote(src, dst, send, recv, axis, index):
    return pltpu.make_async_remote_copy(
        src_ref=src, dst_ref=dst, send_sem=send, recv_sem=recv,
        device_id={axis: index}, device_id_type=MESH,
    )


def greet(devices):
    barrier = pltpu.get_barrier_semaphore()
    for axis, index in devices:
        pl.semaphore_signal(barrier, inc=1, device_id={axis: index}, device_id_type=MESH)
    pl.semaphore_wait(barrier, len(devices))


def project_kernel(
    m, x, wq, wk, wv, cos, sin, ptt,
    q_out, kv_out, mt_out,
    wbuf, own, s1, r1, s2, r2,
    wsem, ss1, rs1, ss2, rs2, ss3, rs3,
):
    nq = q_out.shape[0]
    nkv = kv_out.shape[0] // 2
    hd = q_out.shape[2]
    half = own.shape[1]
    core, partner, peers = place(m)
    parts = chunks_of(nq, 3) + [(nq, 2 * nkv)]
    count = len(parts)
    loads = []
    for i, (h0, n) in enumerate(parts):
        if i < count - 1:
            loads.append([pltpu.make_async_copy(
                wq.at[:, pl.ds(h0 * hd, n * hd)], wbuf.at[:, pl.ds(h0 * hd, n * hd)], wsem.at[i])])
        else:
            loads.append([
                pltpu.make_async_copy(wk, wbuf.at[:, pl.ds(nq * hd, nkv * hd)], wsem.at[i]),
                pltpu.make_async_copy(wv, wbuf.at[:, pl.ds((nq + nkv) * hd, nkv * hd)], wsem.at[i + 1]),
            ])
    for group in loads:
        for load in group:
            load.start()
    greet([("kvp", partner)] + [("kvp", p) for p in peers])
    mine = pl.ds(pl.multiple_of(core * half, half), half)
    other = pl.ds(pl.multiple_of((1 - core) * half, half), half)
    first, second, third = [], [], []

    def stage1(i):
        h0, n = parts[i]
        for load in loads[i]:
            load.wait()
        w = wbuf[:, h0 * hd:(h0 + n) * hd]
        theirs = jnp.dot(x[other, :], w, preferred_element_type=jnp.float32)
        for j in range(n):
            s1[h0 + j] = theirs[:, j * hd:(j + 1) * hd].astype(jnp.bfloat16)
        copy = remote(s1.at[pl.ds(h0, n)], r1.at[pl.ds(h0, n)], ss1.at[i], rs1.at[i], "kvp", partner)
        copy.start()
        first.append(copy)
        ours = jnp.dot(x[mine, :], w, preferred_element_type=jnp.float32)
        for j in range(n):
            own[h0 + j] = ours[:, j * hd:(j + 1) * hd]

    def stage2(i):
        h0, n = parts[i]
        first[i].wait_recv()
        for h in range(h0, h0 + n):
            value = own[h] + r1[h].astype(jnp.float32)
            own[h] = value
            s2[h] = value.astype(jnp.bfloat16)
        group = []
        for s, peer in enumerate(peers):
            copy = remote(
                s2.at[pl.ds(h0, n)], r2.at[s, pl.ds(h0, n)], ss2.at[s, i], rs2.at[s, i], "kvp", peer)
            copy.start()
            group.append(copy)
        second.append(group)

    for i in range(count):
        stage1(i)
        if i:
            stage2(i - 1)
    stage2(count - 1)

    slots, batch = mt_out.shape
    base = lax.axis_index("kvp") * slots
    ids = lax.broadcasted_iota(jnp.int32, (slots, batch), 0) + base

    def mark(j, found):
        row = ptt[pl.ds(j, 1), :]
        return jnp.where(row == ids, j, found)

    mt_out[...] = lax.fori_loop(
        0, ptt.shape[0], mark, jnp.full((slots, batch), -1, jnp.int32), unroll=4)

    cosine = cos[mine, :]
    sine = sin[mine, :]

    def turn(value):
        return (value * cosine + pltpu.roll(value, hd // 2, 1) * sine).astype(jnp.bfloat16)

    for i in range(count):
        h0, n = parts[i]
        for copy in second[i]:
            copy.wait_recv()
        for h in range(h0, h0 + n):
            value = own[h]
            for s in range(len(peers)):
                value = value + r2[s, h].astype(jnp.float32)
            if h < nq:
                q_out[h, mine, :] = turn(value)
            elif h < nq + nkv:
                kv_out[h - nq] = turn(value)
            else:
                kv_out[h - nq] = value.astype(jnp.bfloat16)
        if i < count - 1:
            part = q_out.at[pl.ds(h0, n), mine, :]
            copy = remote(part, part, ss3.at[i], rs3.at[i], "kvp", partner)
            copy.start()
            third.append(copy)
    for copy in first:
        copy.wait_send()
    for group in second:
        for copy in group:
            copy.wait_send()
    for copy in third:
        copy.wait()


def project(m, x, wq, wk, wv, cos, sin, ptt, slots, hd):
    batch, depth = x.shape
    nq = wq.shape[1] // hd
    nkv = wk.shape[1] // hd
    heads = nq + 2 * nkv
    half = batch // 2
    nqc = len(chunks_of(nq, 3))
    vmem = pl.BlockSpec(memory_space=pltpu.VMEM)
    hbm = pl.BlockSpec(memory_space=pl.ANY)
    dma = pltpu.SemaphoreType.DMA
    return pl.pallas_call(
        functools.partial(project_kernel, m),
        out_shape=(
            jax.ShapeDtypeStruct((nq, batch, hd), jnp.bfloat16),
            jax.ShapeDtypeStruct((2 * nkv, half, hd), jnp.bfloat16),
            jax.ShapeDtypeStruct((slots, batch), jnp.int32),
        ),
        in_specs=[vmem, hbm, hbm, hbm, vmem, vmem, vmem],
        out_specs=(vmem, vmem, vmem),
        scratch_shapes=[
            pltpu.VMEM((depth, heads * hd), jnp.bfloat16),
            pltpu.VMEM((heads, half, hd), jnp.float32),
            pltpu.VMEM((heads, half, hd), jnp.bfloat16),
            pltpu.VMEM((heads, half, hd), jnp.bfloat16),
            pltpu.VMEM((heads, half, hd), jnp.bfloat16),
            pltpu.VMEM((m - 1, heads, half, hd), jnp.bfloat16),
            dma((nqc + 2,)), dma((nqc + 1,)), dma((nqc + 1,)),
            dma((m - 1, nqc + 1)), dma((m - 1, nqc + 1)), dma((nqc,)), dma((nqc,)),
        ],
        compiler_params=pltpu.CompilerParams(
            collective_id=0, has_side_effects=True, vmem_limit_bytes=VMEM_LIMIT),
    )(x, wq, wk, wv, cos, sin, ptt)


def finish_kernel(
    m, ntp, o, stats, q, kv, wout, out,
    wbuf, r1o, r1s, mo, s2o, s2s, r2o, r2s, tile, ho, snew, tsend, town, trecv,
    wsem, s1sem, r1sem, s2sem, r2sem, s3sem, r3sem, s4sem, r4sem,
):
    nq, half, hd = mo.shape
    nqp = stats.shape[1] // 2
    core, partner, peers = place(m)
    tp = lax.axis_index("tp")
    load = pltpu.make_async_copy(wout, wbuf, wsem)
    load.start()
    greet(
        [("kvp", partner)] + [("kvp", p) for p in peers]
        + [("tp", (tp + d) % ntp) for d in range(1, ntp)]
    )
    mine = pl.ds(pl.multiple_of(core * half, half), half)
    other = pl.ds(pl.multiple_of((1 - core) * half, half), half)
    parts = chunks_of(nq, 3)
    count = len(parts)
    stat1 = remote(stats.at[1 - core], r1s, s1sem.at[count], r1sem.at[count], "kvp", partner)
    stat1.start()
    first = []
    for i, (h0, n) in enumerate(parts):
        copy = remote(
            o.at[pl.ds(h0, n), other, :], r1o.at[pl.ds(h0, n)], s1sem.at[i], r1sem.at[i], "kvp", partner)
        copy.start()
        first.append(copy)
    nkv = kv.shape[0] // 2
    group = nq // nkv
    ones = jnp.ones((8, hd), jnp.float32)
    snew[...] = jnp.full(snew.shape, NEG, jnp.float32)
    for h in range(nq):
        product = q[h, mine, :].astype(jnp.float32) * kv[h // group].astype(jnp.float32)
        row = lax.dot_general(
            ones, product, (((1,), (1,)), ((), ())),
            precision=lax.Precision.HIGHEST, preferred_element_type=jnp.float32)
        snew[h:h + 1, :] = row[0:1] * (hd ** -0.5)

    def merged(sources):
        top = sources[0][0]
        for t, _ in sources[1:]:
            top = jnp.maximum(top, t)
        raw = [jnp.exp(t - top) * total for t, total in sources]
        total = raw[0]
        for r in raw[1:]:
            total = total + r
        safe = jnp.where(total > 0.0, total, 1.0)
        for k, r in enumerate(raw):
            tile[k * nqp:(k + 1) * nqp, :] = r / safe
        return top, total, tile[...].T

    tile[...] = jnp.zeros(tile.shape, jnp.float32)
    stat1.wait_recv()
    top, total, cols = merged([
        (stats[core, :nqp], stats[core, nqp:]), (r1s[:nqp], r1s[nqp:]),
    ])
    s2s[:nqp] = top
    s2s[nqp:] = total
    stat2 = []
    for s, peer in enumerate(peers):
        copy = remote(s2s, r2s.at[s], s2sem.at[s, count], r2sem.at[s, count], "kvp", peer)
        copy.start()
        stat2.append(copy)
    second = []
    for i, (h0, n) in enumerate(parts):
        first[i].wait_recv()
        for h in range(h0, h0 + n):
            value = (
                cols[:, h:h + 1] * o[h, mine, :].astype(jnp.float32)
                + cols[:, nqp + h:nqp + h + 1] * r1o[h].astype(jnp.float32)
            )
            mo[h] = value
            s2o[h] = value.astype(jnp.bfloat16)
        copies = []
        for s, peer in enumerate(peers):
            copy = remote(
                s2o.at[pl.ds(h0, n)], r2o.at[s, pl.ds(h0, n)], s2sem.at[s, i], r2sem.at[s, i], "kvp", peer)
            copy.start()
            copies.append(copy)
        second.append(copies)
    for copy in stat2:
        copy.wait_recv()
    sources = [(top, total)]
    for s in range(len(peers)):
        sources.append((r2s[s, :nqp], r2s[s, nqp:]))
    sources.append((snew[...], jnp.ones(snew.shape, jnp.float32)))
    _, _, cols = merged(sources)
    last = len(sources) - 1
    third = []
    for i, (h0, n) in enumerate(parts):
        for copy in second[i]:
            copy.wait_recv()
        for h in range(h0, h0 + n):
            value = cols[:, h:h + 1] * mo[h]
            for s in range(len(peers)):
                at = (s + 1) * nqp + h
                value = value + cols[:, at:at + 1] * r2o[s, h].astype(jnp.float32)
            at = last * nqp + h
            value = value + cols[:, at:at + 1] * kv[nkv + h // group].astype(jnp.float32)
            ho[mine, h * hd:(h + 1) * hd] = value.astype(jnp.bfloat16)
        part = ho.at[mine, pl.ds(h0 * hd, n * hd)]
        copy = remote(part, part, s3sem.at[i], r3sem.at[i], "kvp", partner)
        copy.start()
        third.append(copy)
    load.wait()
    for copy in third:
        copy.wait()
    pieces, batch, width = tsend.shape
    rows = batch // ntp
    fourth = []
    keep = pl.ds(pl.multiple_of(tp * rows, rows), rows)
    for j in range(pieces):
        terms = jnp.dot(
            ho[...], wbuf[:, j * width:(j + 1) * width], preferred_element_type=jnp.float32)
        town[...] = terms
        tsend[j] = terms.astype(jnp.bfloat16)
        copies = []
        for d in range(1, ntp):
            to = (tp + d) % ntp
            take = pl.ds(pl.multiple_of(to * rows, rows), rows)
            copy = remote(
                tsend.at[j, take, :], trecv.at[d - 1, j], s4sem.at[d - 1, j], r4sem.at[d - 1, j], "tp", to)
            copy.start()
            copies.append(copy)
        fourth.append(copies)
        mo_piece = town[keep, :]
        wbuf_keep = pl.ds(j * width, width)
        out[:, wbuf_keep] = mo_piece
    for j in range(pieces):
        value = out[:, j * width:(j + 1) * width]
        for d in range(1, ntp):
            fourth[j][d - 1].wait_recv()
            value = value + trecv[d - 1, j].astype(jnp.float32)
        out[:, j * width:(j + 1) * width] = value
    stat1.wait_send()
    for copy in first + stat2:
        copy.wait_send()
    for copies in second + fourth:
        for copy in copies:
            copy.wait_send()


def finish(m, ntp, o, stats, q, kv, wout):
    nq, batch, hd = o.shape
    half = batch // 2
    nqp = stats.shape[1] // 2
    count = len(chunks_of(nq, 3))
    width = wout.shape[1]
    pieces = len(chunks_of(width // hd, 3))
    rows = batch // ntp
    tile_rows = max((m + 1) * nqp, half)
    vmem = pl.BlockSpec(memory_space=pltpu.VMEM)
    hbm = pl.BlockSpec(memory_space=pl.ANY)
    dma = pltpu.SemaphoreType.DMA
    return pl.pallas_call(
        functools.partial(finish_kernel, m, ntp),
        out_shape=jax.ShapeDtypeStruct((rows, width), jnp.float32),
        in_specs=[vmem, vmem, vmem, vmem, hbm],
        out_specs=vmem,
        scratch_shapes=[
            pltpu.VMEM(wout.shape, jnp.bfloat16),
            pltpu.VMEM((nq, half, hd), jnp.bfloat16),
            pltpu.VMEM((2 * nqp, half), jnp.float32),
            pltpu.VMEM((nq, half, hd), jnp.float32),
            pltpu.VMEM((nq, half, hd), jnp.bfloat16),
            pltpu.VMEM((2 * nqp, half), jnp.float32),
            pltpu.VMEM((m - 1, nq, half, hd), jnp.bfloat16),
            pltpu.VMEM((m - 1, 2 * nqp, half), jnp.float32),
            pltpu.VMEM((tile_rows, half), jnp.float32),
            pltpu.VMEM((batch, nq * hd), jnp.bfloat16),
            pltpu.VMEM((nqp, half), jnp.float32),
            pltpu.VMEM((pieces, batch, width // pieces), jnp.bfloat16),
            pltpu.VMEM((batch, width // pieces), jnp.float32),
            pltpu.VMEM((ntp - 1, pieces, rows, width // pieces), jnp.bfloat16),
            dma, dma((count + 1,)), dma((count + 1,)),
            dma((m - 1, count + 1)), dma((m - 1, count + 1)),
            dma((count,)), dma((count,)),
            dma((ntp - 1, pieces)), dma((ntp - 1, pieces)),
        ],
        compiler_params=pltpu.CompilerParams(
            collective_id=1, has_side_effects=True, vmem_limit_bytes=VMEM_LIMIT),
    )(o, stats, q, kv, wout)


def attend(q, mt, lengths, key_cache, value_cache):
    nq, batch, hd = q.shape
    nkv, slots, page, _ = key_cache.shape
    group = nq // nkv
    hit = mt >= 0
    held = jnp.sum(jnp.where(hit, lengths[None, :] - mt * page, 0), axis=1)
    valid = jnp.arange(page, dtype=jnp.int32)[None, :] < held[:, None]
    mask = valid[None, :, None, :]
    owned = jnp.einsum("pb,hbd->hpd", hit.astype(jnp.bfloat16), q)
    owned = owned.reshape(nkv, group, slots, hd)
    scores = jnp.einsum(
        "hgpd,hptd->hpgt", owned, key_cache, preferred_element_type=jnp.float32) * hd ** -0.5
    scores = jnp.where(mask, scores, NEG)
    slot_top = jnp.max(scores, axis=-1)
    weights = jnp.where(mask, jnp.exp(scores - slot_top[..., None]), 0.0)
    slot_total = jnp.sum(weights, axis=-1)
    slot_acc = jnp.einsum(
        "hpgt,hptd->hpgd", weights.astype(jnp.bfloat16), value_cache,
        preferred_element_type=jnp.float32)
    cover = hit[None, :, None, :]
    top = jnp.max(jnp.where(cover, slot_top[..., None], NEG), axis=1)
    factor = jnp.where(cover, jnp.exp(slot_top[..., None] - top[:, None]), 0.0)
    total = jnp.sum(factor * slot_total[..., None], axis=1)
    acc = jnp.einsum("hpgb,hpgd->hgbd", factor, slot_acc, preferred_element_type=jnp.float32)
    safe = jnp.where(total > 0.0, total, 1.0)
    o = (acc / safe[..., None]).astype(jnp.bfloat16).reshape(nq, batch, hd)
    nqp = -(-nq // 8) * 8
    pad = ((0, nqp - nq), (0, 0))
    stats = jnp.concatenate(
        [
            jnp.pad(top.reshape(nq, batch), pad, constant_values=NEG),
            jnp.pad(total.reshape(nq, batch), pad),
        ]
    )
    return o, stats.reshape(2 * nqp, 2, batch // 2).transpose(1, 0, 2)


def body(m, ntp, normed, w_query, w_key, w_value, w_out, key_cache, value_cache, lengths, page_table):
    hd = key_cache.shape[3]
    cos, sin = angles(lengths.astype(jnp.float32), hd)
    q, kv, mt = project(
        m, normed, w_query, w_key, w_value, cos, sin, page_table.T, key_cache.shape[1], hd)
    o, stats = attend(q, mt, lengths, key_cache, value_cache)
    return finish(m, ntp, o, stats, q, kv, w_out).astype(jnp.bfloat16)


def solution(mesh):
    return jax.shard_map(
        functools.partial(body, mesh.shape["kvp"] // 2, mesh.shape["tp"]),
        mesh=mesh,
        in_specs=(
            P("grp", "kvp"),
            P("kvp", "tp"),
            P("kvp", "tp"),
            P("kvp", "tp"),
            P("tp", "kvp"),
            P("tp", ("grp", "kvp"), None, None),
            P("tp", ("grp", "kvp"), None, None),
            P("grp"),
            P("grp", None),
        ),
        out_specs=P(("grp", "tp"), "kvp"),
        check_vma=False,
    )
```

time: 188 us -> 82.9 us (0.44)
  waiting for transfers between devices: 85.7 us -> 0 us
  Pallas kernels: 0 us -> 58.3 us
  blocking collectives: 15.9 us -> 0 us
  matrix products: 30.4 us -> 15.9 us
  local copies, waits for them, and re-layouts: 14.2 us -> 0.6 us
  between operations: 13.5 us -> 0.09 us
  starting transfers between devices: 10.4 us -> 0 us
  other arithmetic: 17.4 us -> 7.63 us
    reduce_scatter x4 -> x0, waiting for transfers between devices: 70.8 us -> none  [the longest x1 36.3 us: body(): lax.psum_scatter(terms, 'tp', scatter_dimension=0, tiled=True)]
    pallas_call x0 -> x2, Pallas kernels: none -> 58.3 us  [the longest x1 37.6 us: finish(): pl.pallas_call(functools.partial(finish_kernel, m, ntp), out_shape=jax.Sh...]
    all_gather x2 -> x0, blocking collectives: 15.9 us -> none  [the longest x1 8.04 us: body(): q_rot = lax.all_gather(q_part, 'kvp', axis=0, tiled=True)]
    all_to_all x3 -> x0, waiting for transfers between devices: 14.9 us -> none  [the longest x1 14.9 us: body(): lax.all_to_all(acc[None], 'kvp', split_axis=1, concat_axis=0, tiled=True)]
    dot_general x8 -> x4, matrix products: 30.4 us -> 15.9 us  [the longest x1 6.9 us: attend(): jnp.einsum('hgpd,hptd->hpgt', owned, key_cache, preferred_element_type=jn...]
    all_to_all x3 -> x0, starting transfers between devices: 10.2 us -> none  [the longest x1 3.56 us: body(): lax.all_to_all(acc[None], 'kvp', split_axis=1, concat_axis=0, tiled=True)]
    unnamed x14 -> x2, local copies, waits for them, and re-layouts: 5.09 us -> 0.01 us
    reduce_or x1 -> x0, other arithmetic: 4.52 us -> none  [body(): present = jnp.any(hits, axis=(0, 1))]
  transfers between devices with their start and end apart: 7 -> 0, of which waited for: 4 -> 0; matrix products, arithmetic and copies ran while one was open for 26% -> 0% of each run, Pallas kernels for 0% -> 0%
where the time goes in v1:
time: 82.9 us; the launch traced here: 82.6 us
  Pallas kernels  58.3 us (70%)
  matrix products  15.9 us (19%)
  other arithmetic  7.63 us (9%)
    pallas_call x1, Pallas kernels, finish(): pl.pallas_call(functools.partial(finish_kernel, m, ntp), out_shape=jax.Sh...  37.6 us
    pallas_call x1, Pallas kernels, project(): pl.pallas_call(functools.partial(project_kernel, m), out_shape=(jax.Shape...  20.7 us
    dot_general x1, matrix products, attend(): jnp.einsum('hgpd,hptd->hpgt', owned, key_cache, preferred_element_type=jn...  6.9 us
    dot_general x1, matrix products, attend(): jnp.einsum('hpgt,hptd->hpgd', weights.astype(jnp.bfloat16), value_cache,...  5.71 us
    dot_general x1, matrix products, attend(): jnp.einsum('hpgb,hpgd->hgbd', factor, slot_acc, preferred_element_type=jn...  1.77 us
    convert_element_type x1, other arithmetic, body(): return finish(m, ntp, o, stats, q, kv, w_out).astype(jnp.bfloat16)  1.69 us

profile of v1, /device:TPU:0, one launch (start us, length us, event | category | flops | bytes accessed | tf_op | source)
XLA Modules:
  0.0 82.6 jit_solution(10063474061995576942)
XLA Ops:
  0.0 0.7 convert_element_type.21
  0.7 0.6 fusion.23
  1.3 0.8 %pad_maximum_fusion = (f32[256,128]{1,0:T(8,128)}, f32[256,128]{1,0:T(8,128)}) fusion(f32[256,64]{1,0:T(8,128)S(1)} %get-tuple-element.15, f32[256,64]{1,0:T(8,128)S(1)} %get-tuple-element.14, f32[256,64]{1,0:T(8,128)S(1)} %get-tuple-element.13), kind=kLoop, calls=%fused_computation.26 | loop fusion | flops 65536 | bytes 458752 | tf_op jit(solution)/shard_map/concatenate | solution.py:30
  2.1 0.0 copy-start
  2.1 20.7 %shard_map.91 = (bf16[12,256,128]{2,1,0:T(8,128)(2,1)}, bf16[4,128,128]{2,1,0:T(8,128)(2,1)}, s32[128,256]{1,0:T(8,128)}) custom-call(bf16[256,1536]{1,0:T(8,128)(2,1)} %x.5, bf16[1536,1536]{1,0:T(8,128)(2,1)} %wq.1, bf16[1536,256]{1,0:T(8,128)(2,1)} %wk.1, bf16[1536,256]{1,0:T(8,128)(2,1)} %wv.1, f32[256,128]{1,0:T(8,128)} %get-tuple-element.18.cos, ...), custom_call_target="tpu_custom_call" | custom-call | tf_op jit(solution)/shard_map/pallas_call | solution.py:187
  22.8 0.0 copy-done
  22.9 1.0 %select_reduce_fusion.1 = (s32[128]{0:T(128)S(1)}, pred[128,256]{1,0:T(32,128)(4,1)S(1)}) fusion(s32[128,256]{1,0:T(8,128)} %get-tuple-element.8, s32[256]{0:T(256)S(1)} %copy-done), kind=kLoop, calls=%fused_computation.28 | loop fusion | flops 163712 | bytes 165376 | tf_op jit(solution)/shard_map/reduce_sum | solution.py:400
  23.9 1.5 %fusion.19 = bf16[12,128,128]{2,1,0:T(8,128)(2,1)S(1)} fusion(bf16[12,256,128]{2,1,0:T(8,128)(2,1)} %get-tuple-element.9.q, pred[128,256]{1,0:T(32,128)(4,1)S(1)} %get-tuple-element.12), kind=kOutput, calls=%fused_computation.29 | convolution fusion | flops 100663296 | bytes 1212416 | tf_op jit(solution)/shard_map/pb,hbd->hpd/dot_general | solution.py:403
  25.4 0.3 copy.30
  25.7 0.1 iota_compare_fusion
  25.8 6.9 %fusion.29 = (f32[2,128,6]{2,1,0:T(8,128)S(1)}, f32[2,128,6,128]{3,2,1,0:T(8,128)S(1)}) fusion(bf16[2,6,128,128]{3,1,2,0:T(8,128)(2,1)S(1)} %copy.30, bf16[2,128,128,128]{3,2,1,0:T(8,128)(2,1)} %param.14, pred[128,128]{1,0:T(8,128)(4,1)S(1)} %iota_compare_fusion), kind=kOutput, calls=%fused_computation.47 | convolution fusion | flops 50919936 | bytes 9590784 | tf_op jit(solution)/shard_map/hgpd,hptd->hpgt/dot_general | solution.py:405
  32.7 0.1 copy.31
  32.8 0.1 copy.28
  32.9 0.5 select_reduce_fusion
  33.4 0.7 fusion.2
  34.1 0.1 copy.33
  34.2 0.9 %multiply_reduce_fusion = f32[2,6,256]{2,1,0:T(8,128)S(1)} fusion(f32[2,128,6]{1,2,0:T(8,128)S(1)} %copy.33, f32[2,6,256]{2,1,0:T(8,128)S(1)} %select_reduce_fusion, f32[2,128,6]{1,2,0:T(8,128)S(1)} %copy.31, pred[128,256]{0,1:T(8,128)(4,1)S(1)} %copy.28), kind=kLoop, calls=%fused_computation.1 | loop fusion | flops 1569792 | bytes 69632 | tf_op jit(solution)/shard_map/reduce_sum | solution.py:417
  35.1 0.6 bitcast_bitcast_fusion.stats
  35.8 5.7 %fusion.9 = bf16[2,128,6,128]{3,2,1,0:T(8,128)(2,1)S(1)} fusion(bf16[2,128,128,128]{3,2,1,0:T(8,128)(2,1)} %param.15, f32[2,128,6,128]{3,2,1,0:T(8,128)S(1)} %get-tuple-element.17, f32[2,128,6]{2,1,0:T(8,128)S(1)} %get-tuple-element.16, pred[128,128]{1,0:T(8,128)(4,1)S(1)} %iota_compare_fusion), kind=kOutput, calls=%fused_computation.15 | convolution fusion | flops 50921472 | bytes 9590784 | tf_op jit(solution)/shard_map/hpgt,hptd->hpgd/dot_general | solution.py:411
  41.5 1.8 %divide_convert_fusion = bf16[2,6,256,128]{3,2,1,0:T(8,128)(2,1)} fusion(bf16[2,128,6,128]{3,2,1,0:T(8,128)(2,1)S(1)} %fusion.9, f32[2,6,256]{2,1,0:T(8,128)S(1)} %compare_select_fusion, f32[2,6,256]{2,1,0:T(8,128)S(1)} %select_reduce_fusion, f32[2,128,6]{1,2,0:T(8,128)S(1)} %copy.31, pred[128,256]{0,1:T(8,128)(4,1)S(1)} %copy.28), kind=kOutput, calls=%fused_computation | convolution fusion | flops 102236160 | bytes 1243136 | tf_op jit(solution)/shard_map/hpgb,hpgd->hgbd/dot_general | solution.py:418
  43.2 37.6 %shard_map.92 = f32[64,1536]{1,0:T(8,128)} custom-call(bf16[12,256,128]{2,1,0:T(8,128)(2,1)} %bitcast.20, f32[2,32,128]{2,1,0:T(8,128)} %bitcast_bitcast_fusion.stats, bf16[12,256,128]{2,1,0:T(8,128)(2,1)} %get-tuple-element.9.q, bf16[4,128,128]{2,1,0:T(8,128)(2,1)} %get-tuple-element.10.kv, bf16[1536,1536]{1,0:T(8,128)(2,1)} %wout.1), custom_call_target="tpu_custom_call" | custom-call | tf_op jit(solution)/shard_map/pallas_call | solution.py:365
  80.9 1.7 %convert_element_type.26 = bf16[64,1536]{1,0:T(8,128)(2,1)} convert(f32[64,1536]{1,0:T(8,128)} %shard_map.92) | non-fusion elementwise | flops 98304 | bytes 589824 | tf_op jit(solution)/shard_map/convert_element_type | solution.py:438
  (6 shorter events, 0.0 us)
Async XLA Ops:
  2.1 20.7 %copy-start = (s32[256]{0:T(256)S(1)}, s32[256]{0:T(256)}, u32[]{:S(2)}) copy-start(s32[256]{0:T(256)} %param.16) | copy-start | bytes 3076

commit v2 on v1

--- a/solution.py
+++ b/solution.py
@@ -17,19 +17,16 @@
 
 def angles(pos, width):
     half = width // 2
-    freq = ROPE_BASE ** (-(2.0 * jnp.arange(half, dtype=jnp.float32)) / width)
+    lane = jnp.arange(width, dtype=jnp.int32)
+    freq = ROPE_BASE ** (-(2.0 * (lane % half).astype(jnp.float32)) / width)
     coarse = lax.optimization_barrier(freq.astype(jnp.bfloat16)).astype(jnp.float32)
     fine = freq - coarse
     pos_e = pos[..., None]
     exact = pos_e * coarse
     turns = jnp.floor(exact / TWO_PI_HIGH)
     angle = exact - turns * TWO_PI_HIGH - turns * TWO_PI_LOW + pos_e * fine
-    cosine = jnp.cos(angle)
-    sine = jnp.sin(angle)
-    return (
-        jnp.concatenate([cosine, cosine], axis=-1),
-        jnp.concatenate([-sine, sine], axis=-1),
-    )
+    sign = jnp.where(lane < half, -1.0, 1.0)
+    return jnp.cos(angle), jnp.sin(angle) * sign
 
 
 def chunks_of(count, most):
@@ -63,8 +60,8 @@
 
 
 def project_kernel(
-    m, x, wq, wk, wv, cos, sin, ptt,
-    q_out, kv_out, mt_out,
+    m, x, wq, wk, wv, cos, sin, ptt, lens,
+    q_out, kv_out, mt_out, owned_out, valid_out,
     wbuf, own, s1, r1, s2, r2,
     wsem, ss1, rs1, ss2, rs2, ss3, rs3,
 ):
@@ -137,8 +134,15 @@
         row = ptt[pl.ds(j, 1), :]
         return jnp.where(row == ids, j, found)
 
-    mt_out[...] = lax.fori_loop(
+    found = lax.fori_loop(
         0, ptt.shape[0], mark, jnp.full((slots, batch), -1, jnp.int32), unroll=4)
+    mt_out[...] = found
+    page = valid_out.shape[1]
+    left = jnp.where(found >= 0, lens[...] - found * page, 0)
+    held = jnp.sum(left, axis=1, keepdims=True)
+    token = lax.broadcasted_iota(jnp.int32, (slots, page), 1)
+    valid_out[...] = jnp.where(token < held, 1, 0)
+    hot = jnp.where(found >= 0, 1.0, 0.0).astype(jnp.bfloat16)
 
     cosine = cos[mine, :]
     sine = sin[mine, :]
@@ -165,16 +169,20 @@
             copy = remote(part, part, ss3.at[i], rs3.at[i], "kvp", partner)
             copy.start()
             third.append(copy)
-    for copy in first:
+    for i, copy in enumerate(third):
+        h0, n = parts[i]
+        copy.wait_recv()
+        for h in range(h0, h0 + n):
+            owned_out[h] = jnp.dot(
+                hot, q_out[h], preferred_element_type=jnp.float32).astype(jnp.bfloat16)
+    for copy in first + third:
         copy.wait_send()
     for group in second:
         for copy in group:
             copy.wait_send()
-    for copy in third:
-        copy.wait()
-
-
-def project(m, x, wq, wk, wv, cos, sin, ptt, slots, hd):
+
+
+def project(m, x, wq, wk, wv, cos, sin, ptt, lens, slots, page, hd):
     batch, depth = x.shape
     nq = wq.shape[1] // hd
     nkv = wk.shape[1] // hd
@@ -190,9 +198,11 @@
             jax.ShapeDtypeStruct((nq, batch, hd), jnp.bfloat16),
             jax.ShapeDtypeStruct((2 * nkv, half, hd), jnp.bfloat16),
             jax.ShapeDtypeStruct((slots, batch), jnp.int32),
+            jax.ShapeDtypeStruct((nq, slots, hd), jnp.bfloat16),
+            jax.ShapeDtypeStruct((slots, page), jnp.int32),
         ),
-        in_specs=[vmem, hbm, hbm, hbm, vmem, vmem, vmem],
-        out_specs=(vmem, vmem, vmem),
+        in_specs=[vmem, hbm, hbm, hbm, vmem, vmem, vmem, vmem],
+        out_specs=(vmem,) * 5,
         scratch_shapes=[
             pltpu.VMEM((depth, heads * hd), jnp.bfloat16),
             pltpu.VMEM((heads, half, hd), jnp.float32),
@@ -205,12 +215,12 @@
         ],
         compiler_params=pltpu.CompilerParams(
             collective_id=0, has_side_effects=True, vmem_limit_bytes=VMEM_LIMIT),
-    )(x, wq, wk, wv, cos, sin, ptt)
+    )(x, wq, wk, wv, cos, sin, ptt, lens)
 
 
 def finish_kernel(
     m, ntp, o, stats, q, kv, wout, out,
-    wbuf, r1o, r1s, mo, s2o, s2s, r2o, r2s, tile, ho, snew, tsend, town, trecv,
+    wbuf, r1o, r1s, mo, s2o, s2s, r2o, r2s, tile, ho, snew, tsend, kept, trecv,
     wsem, s1sem, r1sem, s2sem, r2sem, s3sem, r3sem, s4sem, r4sem,
 ):
     nq, half, hd = mo.shape
@@ -224,17 +234,23 @@
         + [("tp", (tp + d) % ntp) for d in range(1, ntp)]
     )
     mine = pl.ds(pl.multiple_of(core * half, half), half)
-    other = pl.ds(pl.multiple_of((1 - core) * half, half), half)
+    batch = o.shape[1]
+    rows = batch // ntp
     parts = chunks_of(nq, 3)
     count = len(parts)
-    stat1 = remote(stats.at[1 - core], r1s, s1sem.at[count], r1sem.at[count], "kvp", partner)
+    chunks = steps_of(half, batch // ntp)
+    size = half // chunks
+    stat1 = remote(stats.at[1 - core], r1s, s1sem.at[0, count], r1sem.at[0, count], "kvp", partner)
     stat1.start()
-    first = []
-    for i, (h0, n) in enumerate(parts):
-        copy = remote(
-            o.at[pl.ds(h0, n), other, :], r1o.at[pl.ds(h0, n)], s1sem.at[i], r1sem.at[i], "kvp", partner)
-        copy.start()
-        first.append(copy)
+    first = {}
+    for r in range(chunks):
+        theirs = pl.ds(pl.multiple_of((1 - core) * half + r * size, size), size)
+        for i, (h0, n) in enumerate(parts):
+            copy = remote(
+                o.at[pl.ds(h0, n), theirs, :], r1o.at[pl.ds(h0, n), pl.ds(r * size, size), :],
+                s1sem.at[r, i], r1sem.at[r, i], "kvp", partner)
+            copy.start()
+            first[r, i] = copy
     nkv = kv.shape[0] // 2
     group = nq // nkv
     ones = jnp.ones((8, hd), jnp.float32)
@@ -268,26 +284,29 @@
     s2s[nqp:] = total
     stat2 = []
     for s, peer in enumerate(peers):
-        copy = remote(s2s, r2s.at[s], s2sem.at[s, count], r2sem.at[s, count], "kvp", peer)
+        copy = remote(s2s, r2s.at[s], s2sem.at[s, 0, count], r2sem.at[s, 0, count], "kvp", peer)
         copy.start()
         stat2.append(copy)
-    second = []
-    for i, (h0, n) in enumerate(parts):
-        first[i].wait_recv()
-        for h in range(h0, h0 + n):
-            value = (
-                cols[:, h:h + 1] * o[h, mine, :].astype(jnp.float32)
-                + cols[:, nqp + h:nqp + h + 1] * r1o[h].astype(jnp.float32)
-            )
-            mo[h] = value
-            s2o[h] = value.astype(jnp.bfloat16)
-        copies = []
-        for s, peer in enumerate(peers):
-            copy = remote(
-                s2o.at[pl.ds(h0, n)], r2o.at[s, pl.ds(h0, n)], s2sem.at[s, i], r2sem.at[s, i], "kvp", peer)
-            copy.start()
-            copies.append(copy)
-        second.append(copies)
+    second = {}
+    for r in range(chunks):
+        span = pl.ds(r * size, size)
+        ours = pl.ds(pl.multiple_of(core * half + r * size, size), size)
+        part_cols = cols[r * size:(r + 1) * size]
+        for i, (h0, n) in enumerate(parts):
+            first[r, i].wait_recv()
+            for h in range(h0, h0 + n):
+                value = (
+                    part_cols[:, h:h + 1] * o[h, ours, :].astype(jnp.float32)
+                    + part_cols[:, nqp + h:nqp + h + 1] * r1o[h, span, :].astype(jnp.float32)
+                )
+                mo[h, span, :] = value
+                s2o[h, span, :] = value.astype(jnp.bfloat16)
+            for s, peer in enumerate(peers):
+                copy = remote(
+                    s2o.at[pl.ds(h0, n), span, :], r2o.at[s, pl.ds(h0, n), span, :],
+                    s2sem.at[s, r, i], r2sem.at[s, r, i], "kvp", peer)
+                copy.start()
+                second[s, r, i] = copy
     for copy in stat2:
         copy.wait_recv()
     sources = [(top, total)]
@@ -296,58 +315,77 @@
     sources.append((snew[...], jnp.ones(snew.shape, jnp.float32)))
     _, _, cols = merged(sources)
     last = len(sources) - 1
+    pieces, _, width = tsend.shape
     third = []
-    for i, (h0, n) in enumerate(parts):
-        for copy in second[i]:
+
+    def crossing(t, j):
+        return remote(
+            tsend.at[j, pl.ds(t * rows, rows), :], trecv.at[(tp - t + ntp) % ntp - 1, j],
+            s4sem.at[t, j], r4sem.at[(tp - t + ntp) % ntp - 1, j], "tp", t)
+
+    for r in range(chunks):
+        span = pl.ds(r * size, size)
+        part_cols = cols[r * size:(r + 1) * size]
+        halves = []
+        for i, (h0, n) in enumerate(parts):
+            for s in range(len(peers)):
+                second[s, r, i].wait_recv()
+            for h in range(h0, h0 + n):
+                value = part_cols[:, h:h + 1] * mo[h, span, :]
+                for s in range(len(peers)):
+                    at = (s + 1) * nqp + h
+                    value = value + part_cols[:, at:at + 1] * r2o[s, h, span, :].astype(jnp.float32)
+                at = last * nqp + h
+                value = value + part_cols[:, at:at + 1] * kv[nkv + h // group, span, :].astype(jnp.float32)
+                ho[core, span, h * hd:(h + 1) * hd] = value.astype(jnp.bfloat16)
+            part = ho.at[core, span, pl.ds(h0 * hd, n * hd)]
+            copy = remote(part, part, s3sem.at[r, i], r3sem.at[r, i], "kvp", partner)
+            copy.start()
+            halves.append(copy)
+        third.extend(halves)
+        if r == 0:
+            load.wait()
+        for copy in halves:
             copy.wait_recv()
-        for h in range(h0, h0 + n):
-            value = cols[:, h:h + 1] * mo[h]
-            for s in range(len(peers)):
-                at = (s + 1) * nqp + h
-                value = value + cols[:, at:at + 1] * r2o[s, h].astype(jnp.float32)
-            at = last * nqp + h
-            value = value + cols[:, at:at + 1] * kv[nkv + h // group].astype(jnp.float32)
-            ho[mine, h * hd:(h + 1) * hd] = value.astype(jnp.bfloat16)
-        part = ho.at[mine, pl.ds(h0 * hd, n * hd)]
-        copy = remote(part, part, s3sem.at[i], r3sem.at[i], "kvp", partner)
-        copy.start()
-        third.append(copy)
-    load.wait()
-    for copy in third:
-        copy.wait()
-    pieces, batch, width = tsend.shape
-    rows = batch // ntp
-    fourth = []
-    keep = pl.ds(pl.multiple_of(tp * rows, rows), rows)
+        finished = jnp.concatenate([ho[0, span, :], ho[1, span, :]], axis=0)
+        for j in range(pieces):
+            terms = jnp.dot(
+                finished, wbuf[:, j * width:(j + 1) * width], preferred_element_type=jnp.float32)
+            for c in range(2):
+                for k in range(size // rows):
+                    t = (c * half + r * size) // rows + k
+                    block = terms[c * size + k * rows:c * size + (k + 1) * rows]
+                    tsend[j, t * rows:(t + 1) * rows, :] = block.astype(jnp.bfloat16)
+
+                    @pl.when(t == tp)
+                    def _():
+                        kept[:, j * width:(j + 1) * width] = block
+
+                    @pl.when(t != tp)
+                    def _():
+                        crossing(t, j).start()
+
     for j in range(pieces):
-        terms = jnp.dot(
-            ho[...], wbuf[:, j * width:(j + 1) * width], preferred_element_type=jnp.float32)
-        town[...] = terms
-        tsend[j] = terms.astype(jnp.bfloat16)
-        copies = []
+        value = kept[:, j * width:(j + 1) * width]
         for d in range(1, ntp):
-            to = (tp + d) % ntp
-            take = pl.ds(pl.multiple_of(to * rows, rows), rows)
-            copy = remote(
-                tsend.at[j, take, :], trecv.at[d - 1, j], s4sem.at[d - 1, j], r4sem.at[d - 1, j], "tp", to)
-            copy.start()
-            copies.append(copy)
-        fourth.append(copies)
-        mo_piece = town[keep, :]
-        wbuf_keep = pl.ds(j * width, width)
-        out[:, wbuf_keep] = mo_piece
-    for j in range(pieces):
-        value = out[:, j * width:(j + 1) * width]
-        for d in range(1, ntp):
-            fourth[j][d - 1].wait_recv()
+            remote(
+                tsend.at[j, pl.ds(0, rows), :], trecv.at[d - 1, j],
+                s4sem.at[0, j], r4sem.at[d - 1, j], "tp", (tp + d) % ntp).wait_recv()
             value = value + trecv[d - 1, j].astype(jnp.float32)
-        out[:, j * width:(j + 1) * width] = value
+        out[:, j * width:(j + 1) * width] = value.astype(jnp.bfloat16)
     stat1.wait_send()
-    for copy in first + stat2:
+    for copy in list(first.values()) + stat2 + list(second.values()) + third:
         copy.wait_send()
-    for copies in second + fourth:
-        for copy in copies:
-            copy.wait_send()
+    for t in range(ntp):
+        for j in range(pieces):
+
+            @pl.when(t != tp)
+            def _():
+                crossing(t, j).wait_send()
+
+
+def steps_of(half, rows):
+    return 2 if (half // 2) % rows == 0 else 1
 
 
 def finish(m, ntp, o, stats, q, kv, wout):
@@ -359,12 +397,13 @@
     pieces = len(chunks_of(width // hd, 3))
     rows = batch // ntp
     tile_rows = max((m + 1) * nqp, half)
+    chunks = steps_of(half, rows)
     vmem = pl.BlockSpec(memory_space=pltpu.VMEM)
     hbm = pl.BlockSpec(memory_space=pl.ANY)
     dma = pltpu.SemaphoreType.DMA
     return pl.pallas_call(
         functools.partial(finish_kernel, m, ntp),
-        out_shape=jax.ShapeDtypeStruct((rows, width), jnp.float32),
+        out_shape=jax.ShapeDtypeStruct((rows, width), jnp.bfloat16),
         in_specs=[vmem, vmem, vmem, vmem, hbm],
         out_specs=vmem,
         scratch_shapes=[
@@ -377,30 +416,28 @@
             pltpu.VMEM((m - 1, nq, half, hd), jnp.bfloat16),
             pltpu.VMEM((m - 1, 2 * nqp, half), jnp.float32),
             pltpu.VMEM((tile_rows, half), jnp.float32),
-            pltpu.VMEM((batch, nq * hd), jnp.bfloat16),
+            pltpu.VMEM((2, half, nq * hd), jnp.bfloat16),
             pltpu.VMEM((nqp, half), jnp.float32),
             pltpu.VMEM((pieces, batch, width // pieces), jnp.bfloat16),
-            pltpu.VMEM((batch, width // pieces), jnp.float32),
+            pltpu.VMEM((rows, width), jnp.float32),
             pltpu.VMEM((ntp - 1, pieces, rows, width // pieces), jnp.bfloat16),
-            dma, dma((count + 1,)), dma((count + 1,)),
-            dma((m - 1, count + 1)), dma((m - 1, count + 1)),
-            dma((count,)), dma((count,)),
-            dma((ntp - 1, pieces)), dma((ntp - 1, pieces)),
+            dma, dma((chunks, count + 1)), dma((chunks, count + 1)),
+            dma((m - 1, chunks, count + 1)), dma((m - 1, chunks, count + 1)),
+            dma((chunks, count)), dma((chunks, count)),
+            dma((ntp, pieces)), dma((ntp - 1, pieces)),
         ],
         compiler_params=pltpu.CompilerParams(
             collective_id=1, has_side_effects=True, vmem_limit_bytes=VMEM_LIMIT),
     )(o, stats, q, kv, wout)
 
 
-def attend(q, mt, lengths, key_cache, value_cache):
-    nq, batch, hd = q.shape
+def attend(owned, valid, mt, key_cache, value_cache):
+    nq, _, hd = owned.shape
+    batch = mt.shape[1]
     nkv, slots, page, _ = key_cache.shape
     group = nq // nkv
     hit = mt >= 0
-    held = jnp.sum(jnp.where(hit, lengths[None, :] - mt * page, 0), axis=1)
-    valid = jnp.arange(page, dtype=jnp.int32)[None, :] < held[:, None]
     mask = valid[None, :, None, :]
-    owned = jnp.einsum("pb,hbd->hpd", hit.astype(jnp.bfloat16), q)
     owned = owned.reshape(nkv, group, slots, hd)
     scores = jnp.einsum(
         "hgpd,hptd->hpgt", owned, key_cache, preferred_element_type=jnp.float32) * hd ** -0.5
@@ -432,10 +469,11 @@
 def body(m, ntp, normed, w_query, w_key, w_value, w_out, key_cache, value_cache, lengths, page_table):
     hd = key_cache.shape[3]
     cos, sin = angles(lengths.astype(jnp.float32), hd)
-    q, kv, mt = project(
-        m, normed, w_query, w_key, w_value, cos, sin, page_table.T, key_cache.shape[1], hd)
-    o, stats = attend(q, mt, lengths, key_cache, value_cache)
-    return finish(m, ntp, o, stats, q, kv, w_out).astype(jnp.bfloat16)
+    q, kv, mt, owned, valid = project(
+        m, normed, w_query, w_key, w_value, cos, sin, page_table.T, lengths[None, :],
+        key_cache.shape[1], key_cache.shape[2], hd)
+    o, stats = attend(owned, valid > 0, mt, key_cache, value_cache)
+    return finish(m, ntp, o, stats, q, kv, w_out)
 
 
 def solution(mesh):

time: 82.9 us -> 76.9 us (0.928)
  the two profiles are of different devices: /device:TPU:0 before, /device:TPU:9 now
where the time goes in v2:
time: 76.9 us; the launch traced here: 76.6 us
  Pallas kernels  53.5 us (70%)
  matrix products  15.6 us (20%)
  other arithmetic  5.58 us (7%)
  local copies, waits for them, and re-layouts  1.92 us (2%)
    pallas_call x1, Pallas kernels, finish(): pl.pallas_call(functools.partial(finish_kernel, m, ntp), out_shape=jax.Sh...  33.4 us
    pallas_call x1, Pallas kernels, project(): pl.pallas_call(functools.partial(project_kernel, m), out_shape=(jax.Shape...  20.1 us
    dot_general x1, matrix products, attend(): jnp.einsum('hgpd,hptd->hpgt', owned, key_cache, preferred_element_type=jn...  8.07 us
    dot_general x1, matrix products, attend(): jnp.einsum('hpgt,hptd->hpgd', weights.astype(jnp.bfloat16), value_cache,...  5.71 us
    dot_general x1, matrix products, attend(): jnp.einsum('hpgb,hpgd->hgbd', factor, slot_acc, preferred_element_type=jn...  1.76 us
    unnamed x3, local copies, waits for them, and re-layouts  1.62 us

profile of v2, /device:TPU:9, one launch (start us, length us, event | category | flops | bytes accessed | tf_op | source)
XLA Modules:
  0.0 76.6 jit_solution(15954207662911235545)
XLA Ops:
  0.0 0.7 convert_element_type.22
  0.7 1.3 %sine_multiply_fusion = (f32[256,128]{1,0:T(8,128)}, f32[256,128]{1,0:T(8,128)}) fusion(f32[128]{0:T(128)S(1)} %get-tuple-element.19, f32[128]{0:T(128)S(1)} %get-tuple-element.20, f32[128]{0:T(128)S(1)} %convert_element_type.25, f32[256]{0:T(256)S(1)} %convert_element_type.22), kind=kLoop, calls=%fused_computation.27 | loop fusion | flops 327680 | bytes 264704 | tf_op jit(solution)/shard_map/mul | solution.py:29
  2.0 20.1 %shard_map.91 = (bf16[12,256,128]{2,1,0:T(8,128)(2,1)}, bf16[4,128,128]{2,1,0:T(8,128)(2,1)}, s32[128,256]{1,0:T(8,128)}, bf16[12,128,128]{2,1,0:T(8,128)(2,1)}, s32[128,128]{1,0:T(8,128)}) custom-call(bf16[256,1536]{1,0:T(8,128)(2,1)} %x.5, bf16[1536,1536]{1,0:T(8,128)(2,1)} %wq.1, bf16[1536,256]{1,0:T(8,128)(2,1)} %wk.1, bf16[1536,256]{1,0:T(8,128)(2,1)} %wv.1, ...), custom_call_target="tpu_custom_call" | custom-call | tf_op jit(solution)/shard_map/pallas_call | solution.py:195
  22.1 0.9 %broadcast_compare_fusion.1 = pred[128,128]{1,0:T(8,128)(4,1)S(1)} fusion(s32[128,128]{1,0:T(8,128)} %get-tuple-element.11), kind=kLoop, calls=%fused_computation.36 | loop fusion | flops 16384 | bytes 81920 | tf_op jit(solution)/shard_map/gt | solution.py:475
  22.9 0.0 copy-start
  23.0 8.1 %fusion.31 = (f32[2,128,6]{2,1,0:T(8,128)S(1)}, f32[2,128,6,128]{3,2,1,0:T(8,128)S(1)}) fusion(bf16[2,128,128,128]{3,2,1,0:T(8,128)(2,1)} %param.14, bf16[2,6,128,128]{3,2,1,0:T(8,128)(2,1)} %bitcast.14, pred[128,128]{1,0:T(8,128)(4,1)S(1)} %broadcast_compare_fusion.1), kind=kOutput, calls=%fused_computation.48 | convolution fusion | flops 50919936 | bytes 9590784 | tf_op jit(solution)/shard_map/hgpd,hptd->hpgt/dot_general | solution.py:442
  31.0 0.1 copy.19
  31.1 0.0 copy-done
  31.2 0.1 copy.17
  31.3 0.5 select_reduce_fusion
  31.8 0.7 fusion.2
  32.4 0.1 copy.21
  32.5 0.9 %multiply_reduce_fusion = f32[2,6,256]{2,1,0:T(8,128)S(1)} fusion(f32[2,128,6]{1,2,0:T(8,128)S(1)} %copy.21, f32[2,6,256]{2,1,0:T(8,128)S(1)} %select_reduce_fusion, f32[2,128,6]{1,2,0:T(8,128)S(1)} %copy.19, pred[128,256]{0,1:T(8,128)(4,1)S(1)} %copy.17), kind=kLoop, calls=%fused_computation.1 | loop fusion | flops 1569792 | bytes 69632 | tf_op jit(solution)/shard_map/reduce_sum | solution.py:454
  33.5 0.6 bitcast_bitcast_fusion.stats
  34.1 5.7 %fusion.9 = bf16[2,128,6,128]{3,2,1,0:T(8,128)(2,1)S(1)} fusion(bf16[2,128,128,128]{3,2,1,0:T(8,128)(2,1)} %param.15, f32[2,128,6,128]{3,2,1,0:T(8,128)S(1)} %get-tuple-element.18, f32[2,128,6]{2,1,0:T(8,128)S(1)} %get-tuple-element.17, pred[128,128]{1,0:T(8,128)(4,1)S(1)} %broadcast_compare_fusion.1), kind=kOutput, calls=%fused_computation.15 | convolution fusion | flops 50921472 | bytes 9590784 | tf_op jit(solution)/shard_map/hpgt,hptd->hpgd/dot_general | solution.py:448
  39.8 1.8 %divide_convert_fusion = bf16[2,6,256,128]{3,2,1,0:T(8,128)(2,1)} fusion(bf16[2,128,6,128]{3,2,1,0:T(8,128)(2,1)S(1)} %fusion.9, f32[2,6,256]{2,1,0:T(8,128)S(1)} %compare_select_fusion, f32[2,6,256]{2,1,0:T(8,128)S(1)} %select_reduce_fusion, f32[2,128,6]{1,2,0:T(8,128)S(1)} %copy.19, pred[128,256]{0,1:T(8,128)(4,1)S(1)} %copy.17), kind=kOutput, calls=%fused_computation | convolution fusion | flops 102236160 | bytes 1243136 | tf_op jit(solution)/shard_map/hpgb,hpgd->hgbd/dot_general | solution.py:455
  41.6 33.4 %shard_map.92 = bf16[64,1536]{1,0:T(8,128)(2,1)} custom-call(bf16[12,256,128]{2,1,0:T(8,128)(2,1)} %bitcast.13, f32[2,32,128]{2,1,0:T(8,128)} %bitcast_bitcast_fusion.stats, bf16[12,256,128]{2,1,0:T(8,128)(2,1)} %get-tuple-element.13.q, bf16[4,128,128]{2,1,0:T(8,128)(2,1)} %get-tuple-element.14.kv, bf16[1536,1536]{1,0:T(8,128)(2,1)} %wout.1), custom_call_target="tpu_custom_call" | custom-call | tf_op jit(solution)/shard_map/pallas_call | solution.py:404
  75.0 1.6 %copy.32 = bf16[64,1536]{1,0:T(8,128)(2,1)} copy(bf16[64,1536]{1,0:T(8,128)(2,1)} %shard_map.92) | data formatting | bytes 393216
  (7 shorter events, 0.1 us)
Async XLA Ops:
  22.9 8.2 %copy-start = (s32[128,256]{1,0:T(8,128)S(1)}, s32[128,256]{1,0:T(8,128)}, u32[]{:S(2)}) copy-start(s32[128,256]{1,0:T(8,128)} %get-tuple-element.10) | copy-start | bytes 393220
